TPU v7x, 256 devices: a whole 4x4x8 slice. The times are simulated.
256 devices in a mesh: rows: 32 (over y, z), cols: 8 (over x, core).
Axes of the slice: x: 4, y: 4, z: 8, core: 2. Of those that a mesh axis runs over, the one named last changes fastest.
Arguments:
- token_ids: int32 [128, 256], P('rows'), may hold values from 0 to 8191
- keep_mask: int32 [128, 256], P('rows'), may hold values 0 or 1
- remask_order: int32 [32768], P('rows'), may hold values from 0 to 32767, each once
- embed_table: bfloat16 [8192, 1024], P(None, 'cols'), may hold values from -6 to 6
- mask_embed: bfloat16 [1024], P('cols'), may hold values from -4 to 4
- conv_one: bfloat16 [3, 3, 1024, 1024], P(None, None, None, 'cols'), may hold values from -0.0625 to 0.0625
- gain_one: float32 [1024], P('cols'), may hold values from 0.25 to 1.75
- bias_one: float32 [1024], P('cols'), may hold values from -3 to 3
- conv_two: bfloat16 [3, 3, 1024, 1024], P(None, None, None, 'cols'), may hold values from -0.0625 to 0.0625
- gain_two: float32 [1024], P('cols'), may hold values from 0.25 to 1.75
- bias_two: float32 [1024], P('cols'), may hold values from -3 to 3
- head_weight: bfloat16 [1024, 8192], P(None, 'cols'), may hold values from -15.6 to 15.6
Outputs:
- features: bfloat16 [128, 256, 1024], P('rows', None, 'cols')
- token_logp: float32 [128, 256], P('rows', 'cols')
Inputs may be any that keep to these rules, and one draw needn't show every extreme that they name: `remask_order`: each rank appears once.
All inputs are finite; a program needn't handle non-finite values. No bound on the sum of `keep_mask` on one device may be relied on, other than what follows from the above.
Results may differ from a plain program's by a relative error of at most 0.0039.
Values may be sent and summed in bfloat16 or wider, within the bound.
A program may use at most 128 MiB of HBM per device.

v0:
```python
import jax
import jax.numpy as jnp
from jax import lax
from jax.sharding import PartitionSpec as P

C = 1024
GROUPS = 32


def with_halo(value, sides, width):
    for axis, dim in sides:
        count, length = (lax.axis_size(axis), value.shape[dim])
        up = [(i, (i + 1) % count) for i in range(count - 1)]
        down = [(j, i) for i, j in up]
        last = lax.slice_in_dim(value, length - width, length, axis=dim)
        leading = lax.slice_in_dim(value, 0, width, axis=dim)
        before = lax.ppermute(last, axis, up)
        after = lax.ppermute(leading, axis, down)
        value = jnp.concatenate([before, value, after], axis=dim)
    return value


def sent_to_all(value, axis):
    copies = jnp.broadcast_to(value, (lax.axis_size(axis), *value.shape))
    return lax.all_to_all(copies, axis, split_axis=0, concat_axis=0, tiled=True)


def over_copies(value, axis):
    return sent_to_all(value, axis).sum(axis=0)


def together(arrays, axis):
    ends = [0]
    for a in arrays:
        ends.append(ends[-1] + a.size)
    so_far = over_copies(jnp.concatenate([a.ravel() for a in arrays]), axis)
    return tuple((so_far[b:e].reshape(a.shape) for a, b, e in zip(arrays, ends, ends[1:])))


def laid_out(tiles, dim):
    tiles = jnp.moveaxis(tiles, 0, dim)
    lengths = tiles.shape
    return tiles.reshape(*lengths[:dim], lengths[dim] * lengths[dim + 1], *lengths[dim + 2 :])


def gathered_copies(value, axis, dim):
    tiles = sent_to_all(value, axis)
    return laid_out(tiles, dim)


def all_in_one(value, axis):
    leaves = jax.tree.leaves(value)
    order = sorted(range(len(leaves)), key=lambda k: -leaves[k].size)
    width = (1, *leaves[order[0]].shape)[-1]
    lines = [
        jnp.pad(leaves[k].reshape(-1), (0, -leaves[k].size % width)).reshape(-1, width)
        for k in order
    ]
    both, at, found = (sent_to_all(jnp.concatenate(lines), axis), 0, {})
    for k, line in zip(order, lines):
        section = both[:, at : at + len(line)].reshape(len(both), -1)
        found[k] = section[:, : leaves[k].size].reshape(-1, *leaves[k].shape)
        at += len(line)
    numbers = iter(range(len(leaves)))
    return jax.tree.map(lambda _: found[next(numbers)], value)


def folded_in_pairs(pieces, combine):
    while len(jax.tree.leaves(pieces)[0]) > 1:
        pieces = jax.vmap(combine)(
            *(jax.tree.map(lambda part: part[side::2], pieces) for side in (0, 1))
        )
    return jax.tree.map(lambda part: part[0], pieces)


def joined_all(value, axis, combine):
    pieces = all_in_one(value, axis)
    return folded_in_pairs(pieces, combine)


def add_taps(total, weight, piece):
    rows_here = piece.shape[0] - 2
    width = piece.shape[1]
    count = piece.shape[2]
    padded = jnp.pad(piece, ((0, 0), (1, 1), (0, 0)))
    for shift_row in range(3):
        for shift_col in range(3):
            window = padded[
                shift_row : shift_row + rows_here, shift_col : shift_col + width
            ].reshape(-1, count)
            taps = weight[shift_row, shift_col]
            total = total + jnp.dot(window, taps, preferred_element_type=jnp.float32)
    return total


def convolve(field, weight):
    rows_here, width, _ = field.shape
    empty = jnp.zeros((rows_here * width, weight.shape[3]), jnp.float32)
    rimmed = with_halo(field, (("rows", 0),), 1)
    total = add_taps(empty, weight, lax.all_gather(rimmed, "cols", axis=2, tiled=True))
    return total.reshape(rows_here, width, -1)


def group_norm(values, gain, bias, height):
    rows_here, width, channels = values.shape
    group_width = C // GROUPS
    flat = values.reshape(rows_here * width, channels // group_width, group_width)
    population = height * width * group_width
    sums, squares = together(
        (jnp.sum(flat, axis=(0, 2)), jnp.sum(flat * flat, axis=(0, 2))), "rows"
    )
    mean = sums / population
    variance = squares / population - mean * mean
    deviation = flat - mean[None, :, None]
    normed = deviation / jnp.sqrt(variance + 1e-05)[None, :, None]
    return normed.reshape(rows_here, width, channels) * gain + bias


def combine_totals(first, second):
    top = jnp.maximum(first[0], second[0])
    summed = first[1] * jnp.exp(first[0] - top) + second[1] * jnp.exp(second[0] - top)
    return (top, summed, first[2] + second[2])


def local(
    token_ids,
    keep_mask,
    remask_order,
    embed_table,
    mask_embed,
    conv_one,
    gain_one,
    bias_one,
    conv_two,
    gain_two,
    bias_two,
    head_weight,
):
    rows_here, width = token_ids.shape
    height = rows_here * lax.axis_size("rows")
    num_cols = lax.axis_size("cols")
    order = remask_order.reshape(rows_here, width)
    visible = (keep_mask == 1) | (order >= height * width // 2)
    looked = jnp.take(embed_table, token_ids, axis=0)
    start = jnp.where(visible[:, :, None], looked, mask_embed[None, None, :])
    hidden = jax.nn.silu(group_norm(convolve(start, conv_one), gain_one, bias_one, height)).astype(
        jnp.bfloat16
    )
    second = group_norm(convolve(hidden, conv_two), gain_two, bias_two, height)
    features = (start.astype(jnp.float32) + second).astype(jnp.bfloat16)
    vocab_here = head_weight.shape[1]
    piece = gathered_copies(features, "cols", 2)
    count = piece.shape[2]
    logits = jnp.dot(piece.reshape(-1, count), head_weight, preferred_element_type=jnp.float32)
    top = jnp.max(logits, axis=1)
    summed = jnp.sum(jnp.exp(logits - top[:, None]), axis=1)
    offset = lax.axis_index("cols") * vocab_here
    vocab_ids = lax.broadcasted_iota(jnp.int32, (1, vocab_here), 1) + offset
    hits = vocab_ids == token_ids.reshape(-1, 1)
    picked = jnp.sum(jnp.where(hits, logits, 0.0), axis=1)
    top, summed, picked = joined_all((top, summed, picked), "cols", combine_totals)
    logp = (picked - top - jnp.log(summed)).reshape(rows_here, width)
    slice_width = width // num_cols
    token_logp = lax.dynamic_slice_in_dim(
        logp, lax.axis_index("cols") * slice_width, slice_width, 1
    )
    return (features, token_logp)


def solution(mesh):
    in_specs = (
        P("rows", None),
        P("rows", None),
        P("rows"),
        P(None, "cols"),
        P("cols"),
        P(None, None, None, "cols"),
        P("cols"),
        P("cols"),
        P(None, None, None, "cols"),
        P("cols"),
        P("cols"),
        P(None, "cols"),
    )
    out_specs = (P("rows", None, "cols"), P("rows", "cols"))
    return jax.shard_map(local, mesh=mesh, in_specs=in_specs, out_specs=out_specs, check_vma=False)
```

profile of v0, /device:TPU:1, one launch (start us, length us, event | category | flops | bytes accessed | tf_op | source)
XLA Modules:
  0.0 250.8 jit_solution(9500933285625379632)
XLA Ops:
  7.2 0.8 broadcast_compare_fusion
  8.1 0.7 fusion.46
  8.8 0.7 compare_and_fusion
  9.5 4.7 %gather_fusion = bf16[1024,128]{1,0:T(8,128)(2,1)S(1)} fusion(bf16[8192,128]{1,0:T(8,128)(2,1)} %param.15, s32[1024]{0:T(1024)S(1)} %broadcast_clamp_fusion), kind=kCustom, calls=%fused_computation | custom fusion | bytes 528384 | tf_op jit(solution)/shard_map/jit(_take)/gather | solution.py:144
  14.2 0.3 select_select_fusion
  14.6 4.4 %collective-permute-start = (bf16[1,256,128]{2,1,0:T(8,128)(2,1)S(1)}, bf16[1,256,128]{2,1,0:T(8,128)(2,1)S(1)}, u32[]{:S(2)}, u32[]{:S(2)}) collective-permute-start(bf16[1,256,128]{2,1,0:T(8,128)(2,1)S(1)} %get-tuple-element.32), channel_id=1, source_target_pairs={{0,8},{8,16},{16,24},{24,32},{32,40},{40,48},{48,56},{56,64},{64,7... | collective-permute-start | bytes 196616 | tf_op jit(solution)/shard_map/ppermute | solution.py:17
  19.0 1.3 collective-permute-start.1
  20.3 3.9 %collective-permute-done.1 = bf16[1,256,128]{2,1,0:T(8,128)(2,1)S(1)} collective-permute-done((bf16[1,256,128]{2,1,0:T(8,128)(2,1)S(1)}, bf16[1,256,128]{2,1,0:T(8,128)(2,1)S(1)}, u32[]{:S(2)}, u32[]{:S(2)}) %collective-permute-start.1) | collective-permute-done | bytes 65568 | tf_op jit(solution)/shard_map/ppermute | solution.py:18
  24.2 0.8 pad_maximum_fusion
  25.0 38.2 %all-gather.3.cloned.1.call-done = bf16[6,256,1024]{2,1,0:T(8,128)(2,1)} async-done(((bf16[6,256,128]{2,1,0:T(8,128)(2,1)}), bf16[6,256,1024]{2,1,0:T(8,128)(2,1)}) %all-gather.3.cloned.1.call-update) | async-done | bytes 3145744 | tf_op jit(solution)/shard_map/all_gather | solution.py:100
  63.3 13.0 %pad_slice_fusion.6 = (bf16[4,256,1024]{2,1,0:T(8,128)(2,1)S(1)}, bf16[4,256,1024]{2,1,0:T(8,128)(2,1)}, bf16[4,256,1024]{2,1,0:T(8,128)(2,1)}, bf16[4,256,1024]...) fusion(bf16[6,256,1024]{2,1,0:T(8,128)(2,1)} %all-gather.3.clon, ...), kind=kLoop, calls=%fused_computation.12 | loop fusion | bytes 28311552 | tf_op jit(solution)/shard_map/slice | solution.py:88
  76.3 1.8 fusion.21
  78.1 1.8 convolution_add_fusion.15
  79.9 1.8 convolution_add_fusion.14
  81.8 0.7 convolution_add_fusion.13
  82.5 0.7 convolution_add_fusion.12
  83.2 0.7 convolution_add_fusion.11
  84.0 0.7 convolution_add_fusion.10
  84.7 0.7 convolution_add_fusion.9
  85.5 0.7 fusion.48
  86.2 0.1 reduce_sum.104
  86.3 0.1 reduce_sum.82
  86.4 0.1 reduce_sum.105
  86.5 0.1 reduce_sum.83
  86.7 0.1 pad_maximum_fusion.3
  86.8 18.0 %all_to_all.22 = f32[32,1,8]{2,1,0:T(1,128)S(1)} all-to-all(f32[32,1,8]{2,1,0:T(1,128)S(1)} %broadcast_in_dim.60), channel_id=1, replica_groups=mesh['rows'=32,'cols'=8] {'rows'}, dimensions={0} | all-to-all | bytes 2048 | tf_op jit(solution)/shard_map/all_to_all | solution.py:25
  104.8 0.1 slice_multiply_fusion.3
  105.0 0.1 div.45
  105.2 0.1 sub.71
  105.2 0.2 multiply_convert_fusion
  105.5 2.2 collective-permute-start.2
  107.7 1.5 collective-permute-start.3
  109.2 3.5 %collective-permute-done.3 = bf16[1,256,128]{2,1,0:T(8,128)(2,1)S(1)} collective-permute-done((bf16[1,256,128]{2,1,0:T(8,128)(2,1)S(1)}, bf16[1,256,128]{2,1,0:T(8,128)(2,1)S(1)}, u32[]{:S(2)}, u32[]{:S(2)}) %collective-permute-start.3) | collective-permute-done | bytes 65568 | tf_op jit(solution)/shard_map/ppermute | solution.py:18
  112.7 0.8 pad_maximum_fusion.1
  113.5 35.7 %all-gather.5.cloned.1.call-done = bf16[6,256,1024]{2,1,0:T(8,128)(2,1)} async-done(((bf16[6,256,128]{2,1,0:T(8,128)(2,1)}), bf16[6,256,1024]{2,1,0:T(8,128)(2,1)}) %all-gather.5.cloned.1.call-update) | async-done | bytes 3145744 | tf_op jit(solution)/shard_map/all_gather | solution.py:100
  149.2 13.0 %pad_slice_fusion = (bf16[4,256,1024]{2,1,0:T(8,128)(2,1)S(1)}, bf16[4,256,1024]{2,1,0:T(8,128)(2,1)}, bf16[4,256,1024]{2,1,0:T(8,128)(2,1)}, bf16[4,256,1024]{2...) fusion(bf16[6,256,1024]{2,1,0:T(8,128)(2,1)} %all-gather.5.clon, ...), kind=kLoop, calls=%fused_computation.6 | loop fusion | bytes 28311552 | tf_op jit(solution)/shard_map/slice | solution.py:88
  162.2 1.8 fusion.11
  164.0 1.8 convolution_add_fusion.7
  165.9 1.8 convolution_add_fusion.6
  167.7 0.7 convolution_add_fusion.5
  168.4 0.7 convolution_add_fusion.4
  169.2 0.7 convolution_add_fusion.3
  169.9 0.7 convolution_add_fusion.2
  170.7 0.7 convolution_add_fusion.1
  171.4 0.7 fusion.47
  172.2 0.1 reduce_sum.108
  172.3 0.1 reduce_sum.109
  172.4 0.1 reduce_sum.111
  172.5 0.1 reduce_sum.112
  172.7 18.0 %all_to_all.23 = f32[32,1,8]{2,1,0:T(1,128)S(1)} all-to-all(f32[32,1,8]{2,1,0:T(1,128)S(1)} %broadcast_in_dim.61), channel_id=1, replica_groups=mesh['rows'=32,'cols'=8] {'rows'}, dimensions={0} | all-to-all | bytes 2048 | tf_op jit(solution)/shard_map/all_to_all | solution.py:25
  190.8 0.1 slice_multiply_fusion.2
  190.9 0.1 div.52
  191.1 0.1 sub.76
  191.2 0.3 add_convert_fusion
  191.6 1.8 broadcast_in_dim.62
  193.3 6.0 %all-to-all-start.2 = ((bf16[8,4,256,128]{3,2,1,0:T(8,128)(2,1)}), bf16[8,4,256,128]{3,2,1,0:T(8,128)(2,1)}, u32[]{:S(2)}, u32[]{:S(2)}) async-start(bf16[8,4,256,128]{3,2,1,0:T(8,128)(2,1)} %broadcast_in_dim.62), calls=%async_computation.2 | async-start | bytes 4194304 | tf_op jit(solution)/shard_map/all_to_all | solution.py:25
  199.4 26.3 %all-to-all-done.2 = bf16[8,4,256,128]{3,2,1,0:T(8,128)(2,1)} async-done(((bf16[8,4,256,128]{3,2,1,0:T(8,128)(2,1)}), bf16[8,4,256,128]{3,2,1,0:T(8,128)(2,1)}, u32[]{:S(2)}, u32[]{:S(2)}) %all-to-all-start.2) | async-done | bytes 2097184 | tf_op jit(solution)/shard_map/all_to_all | solution.py:25
  225.7 2.9 %copy.22 = bf16[4,256,8,128]{3,2,1,0:T(8,128)(2,1)S(1)} copy(bf16[4,256,8,128]{3,1,0,2:T(8,128)(2,1)} %bitcast.39) | data formatting | bytes 4194304 | tf_op jit(solution)/shard_map/transpose | solution.py:41
  228.7 2.4 fusion.52
  231.1 1.4 exponential_reduce_fusion
  232.5 0.7 broadcast_in_dim.64
  233.2 4.2 %all-to-all-start.3 = ((f32[8,3,1024]{2,1,0:T(4,128)}), f32[8,3,1024]{2,1,0:T(4,128)S(1)}, u32[]{:S(2)}, u32[]{:S(2)}) async-start(f32[8,3,1024]{2,1,0:T(4,128)} %broadcast_in_dim.64), calls=%async_computation.3 | async-start | bytes 262144 | tf_op jit(solution)/shard_map/all_to_all | solution.py:25
  237.4 5.3 %all-to-all-done.3 = f32[8,3,1024]{2,1,0:T(4,128)S(1)} async-done(((f32[8,3,1024]{2,1,0:T(4,128)}), f32[8,3,1024]{2,1,0:T(4,128)S(1)}, u32[]{:S(2)}, u32[]{:S(2)}) %all-to-all-start.3) | async-done | bytes 98336 | tf_op jit(solution)/shard_map/all_to_all | solution.py:25
  243.3 0.7 constant_dynamic-slice_fusion
  (77 shorter events, 1.3 us)
Async XLA Ops:
  7.2 221.5 %copy-start = (bf16[1024,1024]{1,0:T(8,128)(2,1)S(1)}, bf16[1024,1024]{1,0:T(8,128)(2,1)}, u32[]{:S(2)}) copy-start(bf16[1024,1024]{1,0:T(8,128)(2,1)} %param.23) | copy-start | bytes 6291460
  7.2 7.1 %copy-start.11 = (bf16[128]{0:T(256)(128)(2,1)S(1)}, bf16[128]{0:T(256)(128)(2,1)}, u32[]{:S(2)}) copy-start(bf16[128]{0:T(256)(128)(2,1)} %param.16) | copy-start | bytes 772
  7.2 56.1 %all-gather.3.cloned.1.call-start = ((), (), s32[]{:S(2)}) async-start(), calls=%async_computation.4 | async-start | bytes 3538944 | tf_op jit(solution)/shard_map/all_gather | solution.py:100
  14.6 5.7 %collective-permute-start = (bf16[1,256,128]{2,1,0:T(8,128)(2,1)S(1)}, bf16[1,256,128]{2,1,0:T(8,128)(2,1)S(1)}, u32[]{:S(2)}, u32[]{:S(2)}) collective-permute-start(bf16[1,256,128]{2,1,0:T(8,128)(2,1)S(1)} %get-tuple-element.32), channel_id=1, source_target_pairs={{0,8},{8,16},{16,24},{24,32},{32,40},{40,48},{48,56},{56,64},{64,7... | collective-permute-start | bytes 196616 | tf_op jit(solution)/shard_map/ppermute | solution.py:17
  19.0 5.2 %collective-permute-start.1 = (bf16[1,256,128]{2,1,0:T(8,128)(2,1)S(1)}, bf16[1,256,128]{2,1,0:T(8,128)(2,1)S(1)}, u32[]{:S(2)}, u32[]{:S(2)}) collective-permute-start(bf16[1,256,128]{2,1,0:T(8,128)(2,1)S(1)} %get-tuple-element.33), channel_id=1, source_target_pairs={{8,0},{16,8},{24,16},{32,24},{40,32},{48,40},{56,48},{64,56},{72,6... | collective-permute-start | bytes 196616 | tf_op jit(solution)/shard_map/ppermute | solution.py:18
  25.0 124.2 %all-gather.5.cloned.1.call-start = ((), (), s32[]{:S(2)}) async-start(), calls=%async_computation.5 | async-start | bytes 3538944 | tf_op jit(solution)/shard_map/all_gather | solution.py:100
  76.3 1.8 copy-start.5
  78.1 1.9 copy-start.3
  78.1 3.7 %copy-start.7 = (bf16[3,3,1024,128]{3,2,1,0:T(8,128)(2,1)S(1)}, bf16[3,3,1024,128]{3,2,1,0:T(8,128)(2,1)}, u32[]{:S(2)}) copy-start(bf16[3,3,1024,128]{3,2,1,0:T(8,128)(2,1)} %param.17) | copy-start | bytes 7077892
  79.9 1.8 copy-start.1
  85.5 19.8 %copy-start.12 = (f32[128]{0:T(128)S(1)}, f32[128]{0:T(128)}, u32[]{:S(2)}) copy-start(f32[128]{0:T(128)} %param.19) | copy-start | bytes 1540
  85.5 19.8 %copy-start.13 = (f32[128]{0:T(128)S(1)}, f32[128]{0:T(128)}, u32[]{:S(2)}) copy-start(f32[128]{0:T(128)} %param.18) | copy-start | bytes 1540
  105.5 3.7 %collective-permute-start.2 = (bf16[1,256,128]{2,1,0:T(8,128)(2,1)S(1)}, bf16[1,256,128]{2,1,0:T(8,128)(2,1)S(1)}, u32[]{:S(2)}, u32[]{:S(2)}) collective-permute-start(bf16[1,256,128]{2,1,0:T(8,128)(2,1)S(1)} %get-tuple-element.30), channel_id=1, source_target_pairs={{0,8},{8,16},{16,24},{24,32},{32,40},{40,48},{48,56},{56,64},{64,7... | collective-permute-start | bytes 196616 | tf_op jit(solution)/shard_map/ppermute | solution.py:17
  107.7 5.0 %collective-permute-start.3 = (bf16[1,256,128]{2,1,0:T(8,128)(2,1)S(1)}, bf16[1,256,128]{2,1,0:T(8,128)(2,1)S(1)}, u32[]{:S(2)}, u32[]{:S(2)}) collective-permute-start(bf16[1,256,128]{2,1,0:T(8,128)(2,1)S(1)} %get-tuple-element.31), channel_id=1, source_target_pairs={{8,0},{16,8},{24,16},{32,24},{40,32},{48,40},{56,48},{64,56},{72,6... | collective-permute-start | bytes 196616 | tf_op jit(solution)/shard_map/ppermute | solution.py:18
  162.2 1.8 copy-start.6
  164.0 1.9 copy-start.4
  164.0 3.7 %copy-start.8 = (bf16[3,3,1024,128]{3,2,1,0:T(8,128)(2,1)S(1)}, bf16[3,3,1024,128]{3,2,1,0:T(8,128)(2,1)}, u32[]{:S(2)}) copy-start(bf16[3,3,1024,128]{3,2,1,0:T(8,128)(2,1)} %param.20) | copy-start | bytes 7077892
  165.9 1.8 copy-start.2
  171.4 19.8 %copy-start.14 = (f32[128]{0:T(128)S(1)}, f32[128]{0:T(128)}, u32[]{:S(2)}) copy-start(f32[128]{0:T(128)} %param.22) | copy-start | bytes 1540
  171.4 19.8 %copy-start.15 = (f32[128]{0:T(128)S(1)}, f32[128]{0:T(128)}, u32[]{:S(2)}) copy-start(f32[128]{0:T(128)} %param.21) | copy-start | bytes 1540
  191.5 1.8 copy-start.9
  193.3 6.0 %copy-start.10 = (s32[4,256]{1,0:T(4,128)S(1)}, s32[4,256]{1,0:T(4,128)}, u32[]{:S(2)}) copy-start(s32[4,256]{1,0:T(4,128)} %param.12) | copy-start | bytes 12292
  193.3 32.4 %all-to-all-start.2 = ((bf16[8,4,256,128]{3,2,1,0:T(8,128)(2,1)}), bf16[8,4,256,128]{3,2,1,0:T(8,128)(2,1)}, u32[]{:S(2)}, u32[]{:S(2)}) async-start(bf16[8,4,256,128]{3,2,1,0:T(8,128)(2,1)} %broadcast_in_dim.62), calls=%async_computation.2 | async-start | bytes 4194304 | tf_op jit(solution)/shard_map/all_to_all | solution.py:25
  233.2 9.5 %all-to-all-start.3 = ((f32[8,3,1024]{2,1,0:T(4,128)}), f32[8,3,1024]{2,1,0:T(4,128)S(1)}, u32[]{:S(2)}, u32[]{:S(2)}) async-start(f32[8,3,1024]{2,1,0:T(4,128)} %broadcast_in_dim.64), calls=%async_computation.3 | async-start | bytes 262144 | tf_op jit(solution)/shard_map/all_to_all | solution.py:25
Sparse Core Ops, SparseCore 0:
  25.1 38.1 all-gather.2
  113.7 35.5 all-gather.4
where the time goes:
time: 251 us
  waiting for transfers between devices  113 us (45%)
  local copies, waits for them, and re-layouts  38.3 us (15%)
  blocking collectives  36.1 us (14%)
  matrix products  22.1 us (9%)
  starting transfers between devices  19.7 us (8%)
  between operations  14.6 us (6%)
  other arithmetic  7.12 us (3%)
    all_gather x2, waiting for transfers between devices, convolve(): lax.all_gather(rimmed, 'cols', axis=2, tiled=True)  73.9 us
    all_to_all x2, blocking collectives, sent_to_all(): return lax.all_to_all(copies, axis, split_axis=0, concat_axis=0, tiled=True)  36.1 us
    all_to_all x2, waiting for transfers between devices, sent_to_all(): return lax.all_to_all(copies, axis, split_axis=0, concat_axis=0, tiled=True)  31.6 us
    slice x2, local copies, waits for them, and re-layouts, add_taps(): padded[shift_row:shift_row + rows_here, shift_col:shift_col + width]  26 us
    dot_general x18, matrix products, add_taps(): total = total + jnp.dot(window, taps, preferred_element_type=jnp.float32)  19.7 us
    all_to_all x2, starting transfers between devices, sent_to_all(): return lax.all_to_all(copies, axis, split_axis=0, concat_axis=0, tiled=True)  10.3 us
    ppermute x2, waiting for transfers between devices, with_halo(): after = lax.ppermute(leading, axis, down)  7.4 us
    ppermute x2, starting transfers between devices, with_halo(): before = lax.ppermute(last, axis, up)  6.61 us
  transfers between devices with their start and end apart: 8, of which 6 were waited for; matrix products, arithmetic and copies ran while one was open for 0% of the time, Pallas kernels for 0%

commit v1 on v0

--- a/solution.py
+++ b/solution.py
@@ -5,6 +5,24 @@
 
 C = 1024
 GROUPS = 32
+
+
+def gather_around(array, axis, dim):
+    ways, here, step = (lax.axis_size(axis), lax.axis_index(axis), array.shape[dim])
+    lengths = [n * ways if d == dim else n for d, n in enumerate(array.shape)]
+    full = lax.dynamic_update_slice_in_dim(
+        jnp.zeros(lengths, array.dtype), array, here * step, axis=dim
+    )
+    going_up = going_down = array
+    for far in range(1, ways // 2 + 1):
+        going_up = lax.ppermute(going_up, axis, [(d, (d + 1) % ways) for d in range(ways)])
+        full = lax.dynamic_update_slice_in_dim(full, going_up, (here - far) % ways * step, axis=dim)
+        if 2 * far < ways:
+            going_down = lax.ppermute(going_down, axis, [(d, (d - 1) % ways) for d in range(ways)])
+            full = lax.dynamic_update_slice_in_dim(
+                full, going_down, (here + far) % ways * step, axis=dim
+            )
+    return full
 
 
 def with_halo(value, sides, width):
@@ -97,7 +115,7 @@
     rows_here, width, _ = field.shape
     empty = jnp.zeros((rows_here * width, weight.shape[3]), jnp.float32)
     rimmed = with_halo(field, (("rows", 0),), 1)
-    total = add_taps(empty, weight, lax.all_gather(rimmed, "cols", axis=2, tiled=True))
+    total = add_taps(empty, weight, gather_around(rimmed, "cols", 2))
     return total.reshape(rows_here, width, -1)
 
 

time: 251 us -> 232 us (0.924)
  waiting for transfers between devices: 113 us -> 57.9 us
  starting transfers between devices: 19.7 us -> 63.1 us
  between operations: 14.6 us -> 1.19 us
  local copies, waits for them, and re-layouts: 38.3 us -> 46 us
    all_gather x2 -> x0, waiting for transfers between devices: 73.9 us -> none  [convolve(): lax.all_gather(rimmed, 'cols', axis=2, tiled=True)]
    ppermute x0 -> x14, starting transfers between devices: none -> 34.8 us  [the longest x8 18.3 us: gather_around(): lax.ppermute(going_up, axis, [(d, (d + 1) % ways) for d in range(ways)])]
    ppermute x0 -> x14, waiting for transfers between devices: none -> 21.3 us  [the longest x8 21.2 us: gather_around(): lax.ppermute(going_up, axis, [(d, (d + 1) % ways) for d in range(ways)])]
    dynamic_update_slice x0 -> x14, local copies, waits for them, and re-layouts: none -> 9.69 us  [the longest x8 5.85 us: gather_around(): lax.dynamic_update_slice_in_dim(full, going_up, (here - far) % ways * ste...]
    all_to_all x2, starting transfers between devices: 10.3 us -> 17.2 us  [sent_to_all(): return lax.all_to_all(copies, axis, split_axis=0, concat_axis=0, tiled=True)]
    slice x2, local copies, waits for them, and re-layouts: 26 us -> 21.3 us  [add_taps(): padded[shift_row:shift_row + rows_here, shift_col:shift_col + width]]
    ppermute x2, waiting for transfers between devices: 7.4 us -> 3.88 us  [with_halo(): after = lax.ppermute(leading, axis, down)]
  transfers between devices with their start and end apart: 8 -> 20, of which waited for: 6 -> 12; matrix products, arithmetic and copies ran while one was open for 0% -> 4% of each run, Pallas kernels for 0% -> 0%
where the time goes in v1:
time: 232 us; the launch traced here: 231 us
  starting transfers between devices  63.1 us (27%)
  waiting for transfers between devices  57.9 us (25%)
  local copies, waits for them, and re-layouts  46 us (20%)
  blocking collectives  35 us (15%)
  matrix products  21.3 us (9%)
  other arithmetic  6.73 us (3%)
    all_to_all x2, blocking collectives, sent_to_all(): return lax.all_to_all(copies, axis, split_axis=0, concat_axis=0, tiled=True)  35 us
    all_to_all x2, waiting for transfers between devices, sent_to_all(): return lax.all_to_all(copies, axis, split_axis=0, concat_axis=0, tiled=True)  31.6 us
    slice x2, local copies, waits for them, and re-layouts, add_taps(): padded[shift_row:shift_row + rows_here, shift_col:shift_col + width]  21.3 us
    ppermute x8, waiting for transfers between devices, gather_around(): lax.ppermute(going_up, axis, [(d, (d + 1) % ways) for d in range(ways)])  21.2 us
    dot_general x18, matrix products, add_taps(): total = total + jnp.dot(window, taps, preferred_element_type=jnp.float32)  18.9 us
    ppermute x8, starting transfers between devices, gather_around(): lax.ppermute(going_up, axis, [(d, (d + 1) % ways) for d in range(ways)])  18.3 us
    all_to_all x2, starting transfers between devices, sent_to_all(): return lax.all_to_all(copies, axis, split_axis=0, concat_axis=0, tiled=True)  17.2 us
    ppermute x6, starting transfers between devices, gather_around(): lax.ppermute(going_down, axis, [(d, (d - 1) % ways) for d in range(ways)])  16.5 us
  transfers between devices with their start and end apart: 20, of which 12 were waited for; matrix products, arithmetic and copies ran while one was open for 4% of the time, Pallas kernels for 0%

profile of v1, /device:TPU:1, one launch (start us, length us, event | category | flops | bytes accessed | tf_op | source)
XLA Modules:
  0.0 231.2 jit_solution(9607987156133763611)
XLA Ops:
  0.7 0.8 broadcast_compare_fusion
  2.2 0.7 compare_and_fusion
  2.9 4.7 %gather_fusion = bf16[1024,128]{1,0:T(8,128)(2,1)S(1)} fusion(bf16[8192,128]{1,0:T(8,128)(2,1)} %param.15, s32[1024]{0:T(1024)S(1)} %broadcast_clamp_fusion), kind=kCustom, calls=%fused_computation | custom fusion | bytes 528384 | tf_op jit(solution)/shard_map/jit(_take)/gather | solution.py:162
  8.1 4.4 %collective-permute-start = (bf16[1,256,128]{2,1,0:T(8,128)(2,1)S(1)}, bf16[1,256,128]{2,1,0:T(8,128)(2,1)S(1)}, u32[]{:S(2)}, u32[]{:S(2)}) collective-permute-start(bf16[1,256,128]{2,1,0:T(8,128)(2,1)S(1)} %get-tuple-element.36), channel_id=1, source_target_pairs={{0,8},{8,16},{16,24},{24,32},{32,40},{40,48},{48,56},{56,64},{64,7... | collective-permute-start | bytes 196616 | tf_op jit(solution)/shard_map/ppermute | solution.py:35
  12.4 1.3 collective-permute-start.1
  13.7 3.9 %collective-permute-done.1 = bf16[1,256,128]{2,1,0:T(8,128)(2,1)S(1)} collective-permute-done((bf16[1,256,128]{2,1,0:T(8,128)(2,1)S(1)}, bf16[1,256,128]{2,1,0:T(8,128)(2,1)S(1)}, u32[]{:S(2)}, u32[]{:S(2)}) %collective-permute-start.1) | collective-permute-done | bytes 65568 | tf_op jit(solution)/shard_map/ppermute | solution.py:36
  17.6 2.0 broadcast.61.clone
  19.7 1.0 pad_maximum_fusion
  20.6 3.0 %collective-permute-start.2 = (bf16[6,256,128]{2,1,0:T(8,128)(2,1)S(1)}, bf16[6,256,128]{2,1,0:T(8,128)(2,1)S(1)}, u32[]{:S(2)}, u32[]{:S(2)}) collective-permute-start(bf16[6,256,128]{2,1,0:T(8,128)(2,1)S(1)} %get-tuple-element.32), channel_id=1, source_target_pairs={{0,1},{1,2},{2,3},{3,4},{4,5},{5,6},{6,7},{7,0},{8,9},{9,10},{10,1... | collective-permute-start | bytes 1179656 | tf_op jit(solution)/shard_map/ppermute | solution.py:18
  23.6 4.7 %collective-permute-done.2 = bf16[6,256,128]{2,1,0:T(8,128)(2,1)S(1)} collective-permute-done((bf16[6,256,128]{2,1,0:T(8,128)(2,1)S(1)}, bf16[6,256,128]{2,1,0:T(8,128)(2,1)S(1)}, u32[]{:S(2)}, u32[]{:S(2)}) %collective-permute-start.2) | collective-permute-done | bytes 393248 | tf_op jit(solution)/shard_map/ppermute | solution.py:18
  28.3 2.5 %collective-permute-start.4 = (bf16[6,256,128]{2,1,0:T(8,128)(2,1)S(1)}, bf16[6,256,128]{2,1,0:T(8,128)(2,1)S(1)}, u32[]{:S(2)}, u32[]{:S(2)}) collective-permute-start(bf16[6,256,128]{2,1,0:T(8,128)(2,1)S(1)} %collective-permute-done.2), channel_id=1, source_target_pairs={{0,1},{1,2},{2,3},{3,4},{4,5},{5,6},{6,7},{7,0},{8,9},{9,10},{10,1... | collective-permute-start | bytes 1179656 | tf_op jit(solution)/shard_map/ppermute | solution.py:18
  31.0 4.6 %collective-permute-done.4 = bf16[6,256,128]{2,1,0:T(8,128)(2,1)S(1)} collective-permute-done((bf16[6,256,128]{2,1,0:T(8,128)(2,1)S(1)}, bf16[6,256,128]{2,1,0:T(8,128)(2,1)S(1)}, u32[]{:S(2)}, u32[]{:S(2)}) %collective-permute-start.4) | collective-permute-done | bytes 393248 | tf_op jit(solution)/shard_map/ppermute | solution.py:18
  35.5 2.5 %collective-permute-start.6 = (bf16[6,256,128]{2,1,0:T(8,128)(2,1)S(1)}, bf16[6,256,128]{2,1,0:T(8,128)(2,1)}, u32[]{:S(2)}, u32[]{:S(2)}) collective-permute-start(bf16[6,256,128]{2,1,0:T(8,128)(2,1)S(1)} %collective-permute-done.4), channel_id=1, source_target_pairs={{0,1},{1,2},{2,3},{3,4},{4,5},{5,6},{6,7},{7,0},{8,9},{9,10},{10,1... | collective-permute-start | bytes 1179656 | tf_op jit(solution)/shard_map/ppermute | solution.py:18
  38.0 1.8 constant_dynamic-update-slice_fusion.14
  39.8 1.4 collective-permute-start.7
  41.2 1.8 constant_dynamic-update-slice_fusion.13
  43.0 2.3 collective-permute-start.8
  45.3 0.9 constant_dynamic-update-slice_fusion.12
  46.2 0.8 constant_dynamic-update-slice_fusion.11
  47.0 1.8 constant_dynamic-update-slice_fusion.10
  48.8 0.8 constant_dynamic-update-slice_fusion.9
  49.6 0.8 collective-permute-done.8
  50.3 0.8 constant_dynamic-update-slice_fusion.8
  51.2 12.9 %pad_slice_fusion.11 = (bf16[4,256,1024]{2,1,0:T(8,128)(2,1)}, bf16[4,256,1024]{2,1,0:T(8,128)(2,1)S(1)}, bf16[4,256,1024]{2,1,0:T(8,128)(2,1)S(1)}, bf16[4,256,...) fusion(bf16[6,256,1024]{2,1,0:T(8,128)(2,1)} %constant_dynamic-, ...), kind=kLoop, calls=%fused_computation.17 | loop fusion | bytes 28311552 | tf_op jit(solution)/shard_map/slice | solution.py:106
  64.1 2.4 %fusion.34 = f32[1024,128]{1,0:T(8,128)S(1)} fusion(bf16[1024,1024]{1,0:T(8,128)(2,1)} %bitcast.137, bf16[3,3,1024,128]{3,2,1,0:T(8,128)(2,1)} %param.17), kind=kOutput, calls=%fused_computation.57 | convolution fusion | flops 268435456 | bytes 2883584 | tf_op jit(solution)/shard_map/dot_general | solution.py:110
  66.5 1.7 fusion.36
  68.2 0.7 fusion.38
  68.9 0.7 fusion.40
  69.6 0.7 fusion.42
  70.3 0.7 fusion.44
  71.1 0.7 fusion.46
  71.8 0.7 fusion.48
  72.7 0.9 fusion.76
  74.0 19.5 %all_to_all.22 = f32[32,1,8]{2,1,0:T(1,128)S(1)} all-to-all(f32[32,1,8]{2,1,0:T(1,128)S(1)} %broadcast_in_dim.60), channel_id=1, replica_groups=mesh['rows'=32,'cols'=8] {'rows'}, dimensions={0} | all-to-all | bytes 2048 | tf_op jit(solution)/shard_map/all_to_all | solution.py:43
  94.2 1.3 collective-permute-start.10
  95.5 4.2 %collective-permute-start.9 = (bf16[1,256,128]{2,1,0:T(8,128)(2,1)S(1)}, bf16[1,256,128]{2,1,0:T(8,128)(2,1)S(1)}, u32[]{:S(2)}, u32[]{:S(2)}) collective-permute-start(bf16[1,256,128]{2,1,0:T(8,128)(2,1)S(1)} %get-tuple-element.34), channel_id=1, source_target_pairs={{0,8},{8,16},{16,24},{24,32},{32,40},{40,48},{48,56},{56,64},{64,7... | collective-permute-start | bytes 196616 | tf_op jit(solution)/shard_map/ppermute | solution.py:35
  99.7 1.1 collective-permute-done.9
  101.5 4.9 %collective-permute-start.11 = (bf16[6,256,128]{2,1,0:T(8,128)(2,1)S(1)}, bf16[6,256,128]{2,1,0:T(8,128)(2,1)S(1)}, u32[]{:S(2)}, u32[]{:S(2)}) collective-permute-start(bf16[6,256,128]{2,1,0:T(8,128)(2,1)S(1)} %get-tuple-element.30), channel_id=1, source_target_pairs={{0,1},{1,2},{2,3},{3,4},{4,5},{5,6},{6,7},{7,0},{8,9},{9,10},{10,1... | collective-permute-start | bytes 1179656 | tf_op jit(solution)/shard_map/ppermute | solution.py:18
  106.4 3.8 %collective-permute-start.12 = (bf16[6,256,128]{2,1,0:T(8,128)(2,1)S(1)}, bf16[6,256,128]{2,1,0:T(8,128)(2,1)S(1)}, u32[]{:S(2)}, u32[]{:S(2)}) collective-permute-start(bf16[6,256,128]{2,1,0:T(8,128)(2,1)S(1)} %get-tuple-element.30), channel_id=1, source_target_pairs={{0,7},{1,0},{2,1},{3,2},{4,3},{5,4},{6,5},{7,6},{8,15},{9,8},{10,9... | collective-permute-start | bytes 1179656 | tf_op jit(solution)/shard_map/ppermute | solution.py:21
  110.2 1.2 collective-permute-done.11
  111.4 2.2 collective-permute-start.13
  113.6 5.0 %collective-permute-start.14 = (bf16[6,256,128]{2,1,0:T(8,128)(2,1)S(1)}, bf16[6,256,128]{2,1,0:T(8,128)(2,1)S(1)}, u32[]{:S(2)}, u32[]{:S(2)}) collective-permute-start(bf16[6,256,128]{2,1,0:T(8,128)(2,1)S(1)} %collective-permute-done.12), channel_id=1, source_target_pairs={{0,7},{1,0},{2,1},{3,2},{4,3},{5,4},{6,5},{7,6},{8,15},{9,8},{10,9... | collective-permute-start | bytes 1179656 | tf_op jit(solution)/shard_map/ppermute | solution.py:21
  118.6 1.2 collective-permute-done.13
  119.8 1.0 collective-permute-start.15
  120.9 6.2 %collective-permute-start.16 = (bf16[6,256,128]{2,1,0:T(8,128)(2,1)S(1)}, bf16[6,256,128]{2,1,0:T(8,128)(2,1)S(1)}, u32[]{:S(2)}, u32[]{:S(2)}) collective-permute-start(bf16[6,256,128]{2,1,0:T(8,128)(2,1)S(1)} %collective-permute-done.14), channel_id=1, source_target_pairs={{0,7},{1,0},{2,1},{3,2},{4,3},{5,4},{6,5},{7,6},{8,15},{9,8},{10,9... | collective-permute-start | bytes 1179656 | tf_op jit(solution)/shard_map/ppermute | solution.py:21
  127.3 0.9 collective-permute-done.15
  128.8 7.8 %collective-permute-done.17 = bf16[6,256,128]{2,1,0:T(8,128)(2,1)S(1)} collective-permute-done((bf16[6,256,128]{2,1,0:T(8,128)(2,1)S(1)}, bf16[6,256,128]{2,1,0:T(8,128)(2,1)S(1)}, u32[]{:S(2)}, u32[]{:S(2)}) %collective-permute-start.17) | collective-permute-done | bytes 393248 | tf_op jit(solution)/shard_map/ppermute | solution.py:18
  136.8 8.4 %pad_slice_fusion.5 = (bf16[4,256,1024]{2,1,0:T(8,128)(2,1)}, bf16[4,256,1024]{2,1,0:T(8,128)(2,1)S(1)}, bf16[4,256,1024]{2,1,0:T(8,128)(2,1)S(1)}, bf16[4,256,1...) fusion(bf16[6,256,1024]{2,1,0:T(8,128)(2,1)S(1)} %constant_dyna, ...), kind=kLoop, calls=%fused_computation.11 | loop fusion | bytes 28311552 | tf_op jit(solution)/shard_map/slice | solution.py:106
  145.2 1.8 fusion.17
  147.0 1.8 fusion.19
  148.8 1.7 fusion.21
  151.2 0.7 fusion.25
  151.9 0.7 fusion.27
  152.7 0.7 fusion.29
  154.2 0.9 fusion.75
  155.6 15.5 %all_to_all.23 = f32[32,1,8]{2,1,0:T(1,128)S(1)} all-to-all(f32[32,1,8]{2,1,0:T(1,128)S(1)} %broadcast_in_dim.61), channel_id=1, replica_groups=mesh['rows'=32,'cols'=8] {'rows'}, dimensions={0} | all-to-all | bytes 2048 | tf_op jit(solution)/shard_map/all_to_all | solution.py:43
  171.9 1.8 broadcast_in_dim.62
  173.7 13.0 %all-to-all-start.2 = ((bf16[8,4,256,128]{3,2,1,0:T(8,128)(2,1)}), bf16[8,4,256,128]{3,2,1,0:T(8,128)(2,1)}, u32[]{:S(2)}, u32[]{:S(2)}) async-start(bf16[8,4,256,128]{3,2,1,0:T(8,128)(2,1)} %broadcast_in_dim.62), calls=%async_computation.2 | async-start | bytes 4194304 | tf_op jit(solution)/shard_map/all_to_all | solution.py:43
  186.7 26.3 %all-to-all-done.2 = bf16[8,4,256,128]{3,2,1,0:T(8,128)(2,1)} async-done(((bf16[8,4,256,128]{3,2,1,0:T(8,128)(2,1)}), bf16[8,4,256,128]{3,2,1,0:T(8,128)(2,1)}, u32[]{:S(2)}, u32[]{:S(2)}) %all-to-all-start.2) | async-done | bytes 2097184 | tf_op jit(solution)/shard_map/all_to_all | solution.py:43
  213.0 2.9 %copy.22 = bf16[4,256,8,128]{3,2,1,0:T(8,128)(2,1)S(1)} copy(bf16[4,256,8,128]{3,1,0,2:T(8,128)(2,1)} %bitcast.39) | data formatting | bytes 4194304 | tf_op jit(solution)/shard_map/transpose | solution.py:59
  216.0 2.4 %fusion.80 = (f32[1024]{0:T(1024)S(1)}, f32[1024,1024]{0,1:T(8,128)S(1)}) fusion(bf16[1024,1024]{1,0:T(8,128)(2,1)S(1)} %copy-done, bf16[128,8,8,128]{3,2,1,0:T(8,128)(2,1)S(1)} %bitcast.143), kind=kOutput, calls=%fused_computation.143 | convolution fusion | flops 2148531200 | bytes 8392704 | tf_op jit(solution)/shard_map/dot_general | solution.py:172
  218.4 1.4 exponential_reduce_fusion
  220.5 4.2 %all-to-all-start.3 = ((f32[8,3,1024]{2,1,0:T(4,128)}), f32[8,3,1024]{2,1,0:T(4,128)S(1)}, u32[]{:S(2)}, u32[]{:S(2)}) async-start(f32[8,3,1024]{2,1,0:T(4,128)} %broadcast_in_dim.64), calls=%async_computation.3 | async-start | bytes 262144 | tf_op jit(solution)/shard_map/all_to_all | solution.py:43
  224.7 5.3 %all-to-all-done.3 = f32[8,3,1024]{2,1,0:T(4,128)S(1)} async-done(((f32[8,3,1024]{2,1,0:T(4,128)}), f32[8,3,1024]{2,1,0:T(4,128)S(1)}, u32[]{:S(2)}, u32[]{:S(2)}) %all-to-all-start.3) | async-done | bytes 98336 | tf_op jit(solution)/shard_map/all_to_all | solution.py:43
  (117 shorter events, 8.9 us)
Async XLA Ops:
  0.6 215.3 %copy-start = (bf16[1024,1024]{1,0:T(8,128)(2,1)S(1)}, bf16[1024,1024]{1,0:T(8,128)(2,1)}, u32[]{:S(2)}) copy-start(bf16[1024,1024]{1,0:T(8,128)(2,1)} %param.23) | copy-start | bytes 6291460
  0.6 7.0 %copy-start.12 = (bf16[128]{0:T(256)(128)(2,1)S(1)}, bf16[128]{0:T(256)(128)(2,1)}, u32[]{:S(2)}) copy-start(bf16[128]{0:T(256)(128)(2,1)} %param.16) | copy-start | bytes 772
  8.1 5.7 %collective-permute-start = (bf16[1,256,128]{2,1,0:T(8,128)(2,1)S(1)}, bf16[1,256,128]{2,1,0:T(8,128)(2,1)S(1)}, u32[]{:S(2)}, u32[]{:S(2)}) collective-permute-start(bf16[1,256,128]{2,1,0:T(8,128)(2,1)S(1)} %get-tuple-element.36), channel_id=1, source_target_pairs={{0,8},{8,16},{16,24},{24,32},{32,40},{40,48},{48,56},{56,64},{64,7... | collective-permute-start | bytes 196616 | tf_op jit(solution)/shard_map/ppermute | solution.py:35
  12.4 5.2 %collective-permute-start.1 = (bf16[1,256,128]{2,1,0:T(8,128)(2,1)S(1)}, bf16[1,256,128]{2,1,0:T(8,128)(2,1)S(1)}, u32[]{:S(2)}, u32[]{:S(2)}) collective-permute-start(bf16[1,256,128]{2,1,0:T(8,128)(2,1)S(1)} %get-tuple-element.37), channel_id=1, source_target_pairs={{8,0},{16,8},{24,16},{32,24},{40,32},{48,40},{56,48},{64,56},{72,6... | collective-permute-start | bytes 196616 | tf_op jit(solution)/shard_map/ppermute | solution.py:36
  20.6 7.7 %collective-permute-start.2 = (bf16[6,256,128]{2,1,0:T(8,128)(2,1)S(1)}, bf16[6,256,128]{2,1,0:T(8,128)(2,1)S(1)}, u32[]{:S(2)}, u32[]{:S(2)}) collective-permute-start(bf16[6,256,128]{2,1,0:T(8,128)(2,1)S(1)} %get-tuple-element.32), channel_id=1, source_target_pairs={{0,1},{1,2},{2,3},{3,4},{4,5},{5,6},{6,7},{7,0},{8,9},{9,10},{10,1... | collective-permute-start | bytes 1179656 | tf_op jit(solution)/shard_map/ppermute | solution.py:18
  23.6 7.3 %collective-permute-start.3 = (bf16[6,256,128]{2,1,0:T(8,128)(2,1)S(1)}, bf16[6,256,128]{2,1,0:T(8,128)(2,1)}, u32[]{:S(2)}, u32[]{:S(2)}) collective-permute-start(bf16[6,256,128]{2,1,0:T(8,128)(2,1)S(1)} %get-tuple-element.32), channel_id=1, source_target_pairs={{0,7},{1,0},{2,1},{3,2},{4,3},{5,4},{6,5},{7,6},{8,15},{9,8},{10,9... | collective-permute-start | bytes 1179656 | tf_op jit(solution)/shard_map/ppermute | solution.py:21
  28.3 7.2 %copy-start.10 = (bf16[6,256,128]{2,1,0:T(8,128)(2,1)}, bf16[6,256,128]{2,1,0:T(8,128)(2,1)S(1)}, u32[]{:S(2)}) copy-start(bf16[6,256,128]{2,1,0:T(8,128)(2,1)S(1)} %collective-permute-done.2) | copy-start | bytes 1179652
  28.3 7.2 %collective-permute-start.4 = (bf16[6,256,128]{2,1,0:T(8,128)(2,1)S(1)}, bf16[6,256,128]{2,1,0:T(8,128)(2,1)S(1)}, u32[]{:S(2)}, u32[]{:S(2)}) collective-permute-start(bf16[6,256,128]{2,1,0:T(8,128)(2,1)S(1)} %collective-permute-done.2), channel_id=1, source_target_pairs={{0,1},{1,2},{2,3},{3,4},{4,5},{5,6},{6,7},{7,0},{8,9},{9,10},{10,1... | collective-permute-start | bytes 1179656 | tf_op jit(solution)/shard_map/ppermute | solution.py:18
  30.9 8.9 %collective-permute-start.5 = (bf16[6,256,128]{2,1,0:T(8,128)(2,1)}, bf16[6,256,128]{2,1,0:T(8,128)(2,1)S(1)}, u32[]{:S(2)}, u32[]{:S(2)}) collective-permute-start(bf16[6,256,128]{2,1,0:T(8,128)(2,1)} %collective-permute-done.3), channel_id=1, source_target_pairs={{0,7},{1,0},{2,1},{3,2},{4,3},{5,4},{6,5},{7,6},{8,15},{9,8},{10,9... | collective-permute-start | bytes 1179656 | tf_op jit(solution)/shard_map/ppermute | solution.py:21
  35.5 7.5 %collective-permute-start.6 = (bf16[6,256,128]{2,1,0:T(8,128)(2,1)S(1)}, bf16[6,256,128]{2,1,0:T(8,128)(2,1)}, u32[]{:S(2)}, u32[]{:S(2)}) collective-permute-start(bf16[6,256,128]{2,1,0:T(8,128)(2,1)S(1)} %collective-permute-done.4), channel_id=1, source_target_pairs={{0,1},{1,2},{2,3},{3,4},{4,5},{5,6},{6,7},{7,0},{8,9},{9,10},{10,1... | collective-permute-start | bytes 1179656 | tf_op jit(solution)/shard_map/ppermute | solution.py:18
  39.8 8.9 %collective-permute-start.7 = (bf16[6,256,128]{2,1,0:T(8,128)(2,1)S(1)}, bf16[6,256,128]{2,1,0:T(8,128)(2,1)S(1)}, u32[]{:S(2)}, u32[]{:S(2)}) collective-permute-start(bf16[6,256,128]{2,1,0:T(8,128)(2,1)S(1)} %collective-permute-done.5), channel_id=1, source_target_pairs={{0,7},{1,0},{2,1},{3,2},{4,3},{5,4},{6,5},{7,6},{8,15},{9,8},{10,9... | collective-permute-start | bytes 1179656 | tf_op jit(solution)/shard_map/ppermute | solution.py:21
  43.0 7.3 %collective-permute-start.8 = (bf16[6,256,128]{2,1,0:T(8,128)(2,1)}, bf16[6,256,128]{2,1,0:T(8,128)(2,1)S(1)}, u32[]{:S(2)}, u32[]{:S(2)}) collective-permute-start(bf16[6,256,128]{2,1,0:T(8,128)(2,1)} %collective-permute-done.6), channel_id=1, source_target_pairs={{0,1},{1,2},{2,3},{3,4},{4,5},{5,6},{6,7},{7,0},{8,9},{9,10},{10,1... | collective-permute-start | bytes 1179656 | tf_op jit(solution)/shard_map/ppermute | solution.py:18
  64.1 2.5 %copy-start.3 = (bf16[4,256,1024]{2,1,0:T(8,128)(2,1)S(1)}, bf16[4,256,1024]{2,1,0:T(8,128)(2,1)}, u32[]{:S(2)}) copy-start(bf16[4,256,1024]{2,1,0:T(8,128)(2,1)} %get-tuple-element.27) | copy-start | bytes 6291460
  64.1 4.1 %copy-start.7 = (bf16[3,3,1024,128]{3,2,1,0:T(8,128)(2,1)S(1)}, bf16[3,3,1024,128]{3,2,1,0:T(8,128)(2,1)}, u32[]{:S(2)}) copy-start(bf16[3,3,1024,128]{3,2,1,0:T(8,128)(2,1)} %param.17) | copy-start | bytes 7077892
  71.1 1.6 copy-start.5
  72.7 21.4 %copy-start.13 = (f32[128]{0:T(128)S(1)}, f32[128]{0:T(128)}, u32[]{:S(2)}) copy-start(f32[128]{0:T(128)} %param.19) | copy-start | bytes 1540
  72.7 21.4 %copy-start.14 = (f32[128]{0:T(128)S(1)}, f32[128]{0:T(128)}, u32[]{:S(2)}) copy-start(f32[128]{0:T(128)} %param.18) | copy-start | bytes 1540
  94.2 5.5 %collective-permute-start.10 = (bf16[1,256,128]{2,1,0:T(8,128)(2,1)S(1)}, bf16[1,256,128]{2,1,0:T(8,128)(2,1)S(1)}, u32[]{:S(2)}, u32[]{:S(2)}) collective-permute-start(bf16[1,256,128]{2,1,0:T(8,128)(2,1)S(1)} %get-tuple-element.35), channel_id=1, source_target_pairs={{8,0},{16,8},{24,16},{32,24},{40,32},{48,40},{56,48},{64,56},{72,6... | collective-permute-start | bytes 196616 | tf_op jit(solution)/shard_map/ppermute | solution.py:36
  95.5 5.3 %collective-permute-start.9 = (bf16[1,256,128]{2,1,0:T(8,128)(2,1)S(1)}, bf16[1,256,128]{2,1,0:T(8,128)(2,1)S(1)}, u32[]{:S(2)}, u32[]{:S(2)}) collective-permute-start(bf16[1,256,128]{2,1,0:T(8,128)(2,1)S(1)} %get-tuple-element.34), channel_id=1, source_target_pairs={{0,8},{8,16},{16,24},{24,32},{32,40},{40,48},{48,56},{56,64},{64,7... | collective-permute-start | bytes 196616 | tf_op jit(solution)/shard_map/ppermute | solution.py:35
  101.5 9.9 %collective-permute-start.11 = (bf16[6,256,128]{2,1,0:T(8,128)(2,1)S(1)}, bf16[6,256,128]{2,1,0:T(8,128)(2,1)S(1)}, u32[]{:S(2)}, u32[]{:S(2)}) collective-permute-start(bf16[6,256,128]{2,1,0:T(8,128)(2,1)S(1)} %get-tuple-element.30), channel_id=1, source_target_pairs={{0,1},{1,2},{2,3},{3,4},{4,5},{5,6},{6,7},{7,0},{8,9},{9,10},{10,1... | collective-permute-start | bytes 1179656 | tf_op jit(solution)/shard_map/ppermute | solution.py:18
  106.4 7.2 %collective-permute-start.12 = (bf16[6,256,128]{2,1,0:T(8,128)(2,1)S(1)}, bf16[6,256,128]{2,1,0:T(8,128)(2,1)S(1)}, u32[]{:S(2)}, u32[]{:S(2)}) collective-permute-start(bf16[6,256,128]{2,1,0:T(8,128)(2,1)S(1)} %get-tuple-element.30), channel_id=1, source_target_pairs={{0,7},{1,0},{2,1},{3,2},{4,3},{5,4},{6,5},{7,6},{8,15},{9,8},{10,9... | collective-permute-start | bytes 1179656 | tf_op jit(solution)/shard_map/ppermute | solution.py:21
  111.4 8.4 %collective-permute-start.13 = (bf16[6,256,128]{2,1,0:T(8,128)(2,1)S(1)}, bf16[6,256,128]{2,1,0:T(8,128)(2,1)S(1)}, u32[]{:S(2)}, u32[]{:S(2)}) collective-permute-start(bf16[6,256,128]{2,1,0:T(8,128)(2,1)S(1)} %collective-permute-done.11), channel_id=1, source_target_pairs={{0,1},{1,2},{2,3},{3,4},{4,5},{5,6},{6,7},{7,0},{8,9},{9,10},{10,1... | collective-permute-start | bytes 1179656 | tf_op jit(solution)/shard_map/ppermute | solution.py:18
  113.6 7.3 %collective-permute-start.14 = (bf16[6,256,128]{2,1,0:T(8,128)(2,1)S(1)}, bf16[6,256,128]{2,1,0:T(8,128)(2,1)S(1)}, u32[]{:S(2)}, u32[]{:S(2)}) collective-permute-start(bf16[6,256,128]{2,1,0:T(8,128)(2,1)S(1)} %collective-permute-done.12), channel_id=1, source_target_pairs={{0,7},{1,0},{2,1},{3,2},{4,3},{5,4},{6,5},{7,6},{8,15},{9,8},{10,9... | collective-permute-start | bytes 1179656 | tf_op jit(solution)/shard_map/ppermute | solution.py:21
  119.8 8.4 %collective-permute-start.15 = (bf16[6,256,128]{2,1,0:T(8,128)(2,1)S(1)}, bf16[6,256,128]{2,1,0:T(8,128)(2,1)S(1)}, u32[]{:S(2)}, u32[]{:S(2)}) collective-permute-start(bf16[6,256,128]{2,1,0:T(8,128)(2,1)S(1)} %collective-permute-done.13), channel_id=1, source_target_pairs={{0,1},{1,2},{2,3},{3,4},{4,5},{5,6},{6,7},{7,0},{8,9},{9,10},{10,1... | collective-permute-start | bytes 1179656 | tf_op jit(solution)/shard_map/ppermute | solution.py:18
  120.9 7.7 %collective-permute-start.16 = (bf16[6,256,128]{2,1,0:T(8,128)(2,1)S(1)}, bf16[6,256,128]{2,1,0:T(8,128)(2,1)S(1)}, u32[]{:S(2)}, u32[]{:S(2)}) collective-permute-start(bf16[6,256,128]{2,1,0:T(8,128)(2,1)S(1)} %collective-permute-done.14), channel_id=1, source_target_pairs={{0,7},{1,0},{2,1},{3,2},{4,3},{5,4},{6,5},{7,6},{8,15},{9,8},{10,9... | collective-permute-start | bytes 1179656 | tf_op jit(solution)/shard_map/ppermute | solution.py:21
  128.2 8.4 %collective-permute-start.17 = (bf16[6,256,128]{2,1,0:T(8,128)(2,1)S(1)}, bf16[6,256,128]{2,1,0:T(8,128)(2,1)S(1)}, u32[]{:S(2)}, u32[]{:S(2)}) collective-permute-start(bf16[6,256,128]{2,1,0:T(8,128)(2,1)S(1)} %collective-permute-done.15), channel_id=1, source_target_pairs={{0,1},{1,2},{2,3},{3,4},{4,5},{5,6},{6,7},{7,0},{8,9},{9,10},{10,1... | collective-permute-start | bytes 1179656 | tf_op jit(solution)/shard_map/ppermute | solution.py:18
  145.2 1.8 copy-start.4
  145.2 3.6 %copy-start.2 = (bf16[4,256,1024]{2,1,0:T(8,128)(2,1)S(1)}, bf16[4,256,1024]{2,1,0:T(8,128)(2,1)}, u32[]{:S(2)}) copy-start(bf16[4,256,1024]{2,1,0:T(8,128)(2,1)} %get-tuple-element.16) | copy-start | bytes 6291460
  147.0 3.5 %copy-start.1 = (bf16[4,256,1024]{2,1,0:T(8,128)(2,1)S(1)}, bf16[4,256,1024]{2,1,0:T(8,128)(2,1)}, u32[]{:S(2)}) copy-start(bf16[4,256,1024]{2,1,0:T(8,128)(2,1)} %get-tuple-element.15) | copy-start | bytes 6291460
  147.0 3.5 %copy-start.8 = (bf16[3,3,1024,128]{3,2,1,0:T(8,128)(2,1)S(1)}, bf16[3,3,1024,128]{3,2,1,0:T(8,128)(2,1)}, u32[]{:S(2)}) copy-start(bf16[3,3,1024,128]{3,2,1,0:T(8,128)(2,1)} %param.20) | copy-start | bytes 7077892
  152.6 1.6 copy-start.6
  154.2 17.3 %copy-start.15 = (f32[128]{0:T(128)S(1)}, f32[128]{0:T(128)}, u32[]{:S(2)}) copy-start(f32[128]{0:T(128)} %param.22) | copy-start | bytes 1540
  154.2 17.3 %copy-start.16 = (f32[128]{0:T(128)S(1)}, f32[128]{0:T(128)}, u32[]{:S(2)}) copy-start(f32[128]{0:T(128)} %param.21) | copy-start | bytes 1540
  171.9 1.8 copy-start.9
  173.7 13.0 %copy-start.11 = (s32[4,256]{1,0:T(4,128)S(1)}, s32[4,256]{1,0:T(4,128)}, u32[]{:S(2)}) copy-start(s32[4,256]{1,0:T(4,128)} %param.12) | copy-start | bytes 12292
  173.7 39.3 %all-to-all-start.2 = ((bf16[8,4,256,128]{3,2,1,0:T(8,128)(2,1)}), bf16[8,4,256,128]{3,2,1,0:T(8,128)(2,1)}, u32[]{:S(2)}, u32[]{:S(2)}) async-start(bf16[8,4,256,128]{3,2,1,0:T(8,128)(2,1)} %broadcast_in_dim.62), calls=%async_computation.2 | async-start | bytes 4194304 | tf_op jit(solution)/shard_map/all_to_all | solution.py:43
  220.5 9.5 %all-to-all-start.3 = ((f32[8,3,1024]{2,1,0:T(4,128)}), f32[8,3,1024]{2,1,0:T(4,128)S(1)}, u32[]{:S(2)}, u32[]{:S(2)}) async-start(f32[8,3,1024]{2,1,0:T(4,128)} %broadcast_in_dim.64), calls=%async_computation.3 | async-start | bytes 262144 | tf_op jit(solution)/shard_map/all_to_all | solution.py:43
